TPU v7x, 32 devices: a whole 2x2x4 slice. The times are simulated.
32 devices in a mesh: groups: 2 (over y), ctx: 8 (over z, x), head: 2 (over core).
Axes of the slice: x: 2, y: 2, z: 4, core: 2. Of those that a mesh axis runs over, the one named last changes fastest.
Arguments:
- queries: bfloat16 [16, 128, 64, 192], P(('groups', 'ctx'), None, 'head'), parts along dimension 0, may hold values from -360 to 360
- latent_pages: bfloat16 [16, 8, 64, 576], P(('groups', 'ctx'), 'head'), parts along dimension 0, may hold values from -6 to 6
- page_scales: bfloat16 [16, 8, 4, 64], P(('groups', 'ctx'), 'head'), parts along dimension 0, may hold values from 0.5 to 2
- page_table: int32 [16, 8], P(('groups', 'ctx')), parts along dimension 0, may hold values from 0 to 7, each once within a row
- lengths: int32 [16], P(('groups', 'ctx')), parts along dimension 0, may hold values from 128 to 512, as said below
- w_keys: bfloat16 [512, 64, 128], P('ctx', 'head'), may hold values from -0.5 to 0.5
- w_values: bfloat16 [512, 64, 128], P('ctx', 'head'), may hold values from -1 to 1
Outputs:
- attended: bfloat16 [16, 128, 64, 128], P(('groups', 'ctx'), None, 'head'), parts along dimension 0
There are 2 independent parts, one for each index of `groups`. A program takes and returns all parts, laid end to end along the dimension named above; an argument that names none is the same for every part. Nothing has to cross between parts.
Inputs may be any that keep to these rules, and one draw needn't show every extreme that they name: `page_table`: each row is a permutation of 0 to 7. `lengths`: a length counts the cached tokens and the 128 rows of the span, which take the last positions; the longest request of a part has exactly 512 tokens.
All inputs are finite; a program needn't handle non-finite values.
Results may differ from a plain program's by a relative error of at most 0.0084.
Values may be sent and summed in bfloat16 or wider, within the bound.
A program may use at most 64 MiB of HBM per device.

v0:
```python
import math

import jax
import jax.numpy as jnp
from jax import lax
from jax.sharding import PartitionSpec as P

NEGATIVE = -1e30


def attend_block(
    running, span_query, page_data, page_factor, first_key, row_offset, up_keys, up_values
):
    row_top, row_total, summed = running
    latent_width = up_keys.shape[0]
    group_count = page_factor.shape[1]
    page_rows = page_data.shape[1]
    key_count = page_data.shape[0] * page_rows
    head_count = span_query.shape[1]
    code_values = page_data[:, :, :latent_width].astype(jnp.float32)
    code_values = code_values.reshape(
        page_data.shape[0], page_rows, group_count, latent_width // group_count
    )
    factor = jnp.swapaxes(page_factor, 1, 2).astype(jnp.float32)[..., None]
    latent = (code_values * factor).reshape(key_count, latent_width).astype(jnp.bfloat16)
    rotary = page_data[:, :, latent_width:].reshape(key_count, -1)
    key_nope = jnp.dot(latent, up_keys, preferred_element_type=jnp.float32).astype(jnp.bfloat16)
    key_nope = key_nope.reshape(key_count, head_count, -1)
    value_rows = jnp.dot(latent, up_values, preferred_element_type=jnp.float32).astype(jnp.bfloat16)
    value_rows = value_rows.reshape(key_count, head_count, -1)
    nope_width = key_nope.shape[2]
    scores = jnp.einsum(
        "chn,khn->hck", span_query[:, :, :nope_width], key_nope, preferred_element_type=jnp.float32
    )
    scores = scores + jnp.einsum(
        "chr,kr->hck", span_query[:, :, nope_width:], rotary, preferred_element_type=jnp.float32
    )
    scores = scores * (1.0 / math.sqrt(span_query.shape[2]))
    row_position = lax.broadcasted_iota(jnp.int32, (span_query.shape[0], key_count), 0)
    key_position = first_key + lax.broadcasted_iota(jnp.int32, (span_query.shape[0], key_count), 1)
    visible = (key_position <= row_offset + row_position)[None]
    new_top = jnp.maximum(row_top, jnp.max(jnp.where(visible, scores, NEGATIVE), axis=2))
    raw_weight = jnp.where(visible, jnp.exp(scores - new_top[..., None]), 0.0)
    rescale = jnp.exp(row_top - new_top)
    row_total = row_total * rescale + jnp.sum(raw_weight, axis=2)
    weights = raw_weight.astype(jnp.bfloat16)
    summed = summed * jnp.swapaxes(rescale, 0, 1)[..., None] + jnp.einsum(
        "hck,khv->chv", weights, value_rows, preferred_element_type=jnp.float32
    )
    return (new_top, row_total, summed)


def sweep(span_query, row_offset, first_block, stop_block, fetch, up_keys, up_values):
    row_count = span_query.shape[0]
    head_count = span_query.shape[1]
    value_width = up_values.shape[1] // head_count
    initial = (
        jnp.full((head_count, row_count), NEGATIVE, jnp.float32),
        jnp.zeros((head_count, row_count), jnp.float32),
        jnp.zeros((row_count, head_count, value_width), jnp.float32),
    )

    def advance(block_index, running):
        page_data, page_factor, first_key = fetch(block_index)
        return attend_block(
            running, span_query, page_data, page_factor, first_key, row_offset, up_keys, up_values
        )

    return lax.fori_loop(first_block, stop_block, advance, initial)


def finish(row_total, summed):
    return (summed / jnp.swapaxes(row_total, 0, 1)[..., None]).astype(jnp.bfloat16)[None]


def on_device(queries, latent_pages, page_scales, page_table, lengths, w_keys, w_values):
    pool_pages, pool_scales = (
        lax.all_gather(latent_pages, "head", axis=1, tiled=True),
        lax.all_gather(page_scales, "head", axis=1, tiled=True),
    )
    full_keys, full_values = (
        lax.all_gather(w_keys, "ctx", axis=0, tiled=True),
        lax.all_gather(w_values, "ctx", axis=0, tiled=True),
    )
    latent_width = full_keys.shape[0]
    up_keys = full_keys.reshape(latent_width, -1)
    up_values = full_values.reshape(latent_width, -1)
    span_query = queries[0]
    own_pages = pool_pages[0]
    own_scales = pool_scales[0]
    own_table = page_table[0]
    row_count = span_query.shape[0]
    block_keys = 2 * own_pages.shape[1]
    own_length = lengths[0]
    block_count = (own_length + block_keys - 1) // block_keys

    def own_fetch(block_index):
        pool_slots = lax.dynamic_slice_in_dim(own_table, 2 * block_index, 2)
        return (
            jnp.take(own_pages, pool_slots, axis=0),
            jnp.take(own_scales, pool_slots, axis=0),
            block_index * block_keys,
        )

    row_top, row_total, summed = sweep(
        span_query, own_length - row_count, 0, block_count, own_fetch, up_keys, up_values
    )
    return finish(row_total, summed)


def solution(mesh):
    return jax.shard_map(
        on_device,
        mesh=mesh,
        in_specs=(
            P(("groups", "ctx"), None, "head", None),
            P(("groups", "ctx"), "head", None, None),
            P(("groups", "ctx"), "head", None, None),
            P(("groups", "ctx"), None),
            P(("groups", "ctx")),
            P("ctx", "head", None),
            P("ctx", "head", None),
        ),
        out_specs=P(("groups", "ctx"), None, "head", None),
        check_vma=False,
    )
```

profile of v0, /device:TPU:26, one launch (start us, length us, event | category | flops | bytes accessed | tf_op | source)
XLA Modules:
  0.0 260.8 jit_solution(5370690594181181261)
XLA Ops:
  6.5 0.7 all-gather.5.cloned.1.call-update
  7.3 0.7 all-gather.3.cloned.1.call-update
  8.7 3.8 %copy.25 = bf16[1,128,32,192]{3,1,2,0:T(8,128)(2,1)} copy(bf16[1,128,32,192]{1,3,2,0:T(8,128)(2,1)} %param.9) | data formatting | bytes 3145728 | tf_op args[0]
  12.5 1.8 all_gather.13
  14.3 2.4 all_gather.12
  16.7 64.1 %all-gather.5.cloned.1.call-done = bf16[512,32,128]{2,1,0:T(8,128)(2,1)} async-done(((bf16[64,32,128]{2,1,0:T(8,128)(2,1)}), bf16[512,32,128]{2,1,0:T(8,128)(2,1)}) %all-gather.5.cloned.1.call-update) | async-done | bytes 4194320 | tf_op jit(solution)/shard_map/all_gather | solution.py:83
  80.9 8.3 %copy.44 = bf16[64,8,32,128]{3,1,2,0:T(8,128)(2,1)} copy(bf16[64,8,32,128]{3,2,1,0:T(8,128)(2,1)} %bitcast.95) | data formatting | bytes 8388608
  89.2 65.2 %all-gather.3.cloned.1.call-done = bf16[512,32,128]{2,1,0:T(8,128)(2,1)} async-done(((bf16[64,32,128]{2,1,0:T(8,128)(2,1)}), bf16[512,32,128]{2,1,0:T(8,128)(2,1)}) %all-gather.3.cloned.1.call-update) | async-done | bytes 4194320 | tf_op jit(solution)/shard_map/all_gather | solution.py:82
  154.3 8.3 %copy.45 = bf16[64,8,32,128]{3,1,2,0:T(8,128)(2,1)} copy(bf16[64,8,32,128]{3,2,1,0:T(8,128)(2,1)} %bitcast.96) | data formatting | bytes 8388608
  162.6 1.6 broadcast_in_dim.59
  164.3 85.7 %while.14 = (s32[]{:T(128)}, f32[32,128]{1,0:T(8,128)S(1)}, f32[32,128]{1,0:T(8,128)S(1)}, f32[128,32,128]{0,2,1:T(8,128)}, s32[]{:T(128)}, /*index=5*/s32[]{:T(...) while((s32[]{:T(128)}, f32[32,128]{1,0:T(8,128)S(1)}, ...), condition=%wide.region_3.4_spmd, body=%wide.region_0.3_spmd.sunk | while | flops 1416927488 | bytes 53806432 | solution.py:69
  164.6 1.7 gather_fusion
  166.4 0.6 gather_fusion.1
  167.4 2.9 %fusion.46 = bf16[16,32,8,128]{3,2,1,0:T(8,128)(2,1)S(1)} fusion(bf16[128,512]{1,0:T(8,128)(2,1)S(1)} %fusion.45, bf16[512,4096]{1,0:T(8,128)(2,1)} %get-tuple-element.236), kind=kOutput, calls=%fused_computation.11.clone.1 | convolution fusion | flops 537395200 | bytes 5373952 | tf_op jit(solution)/shard_map/while/body/dot_general | solution.py:27
  170.3 3.3 %copy.53 = bf16[128,32,192]{0,2,1:T(8,128)(2,1)S(1)} copy(bf16[128,32,192]{2,0,1:T(8,128)(2,1)} %get-tuple-element.237) | data formatting | bytes 3145728 | tf_op jit(solution)/shard_map
  173.6 1.7 fusion.44
  175.4 2.9 %select_reduce_fusion.2 = (f32[32,128]{1,0:T(8,128)S(1)}, f32[32,128,128]{1,2,0:T(8,128)S(1)}) fusion(pred[128,128]{0,1:T(8,128)(4,1)S(1)} %broadcast_compare_fusion.2, f32[128,128,32]{1,0,2:T(8,128)} %fusion.44, bf16[128,32,192]{2,0,1:T(8,128)(2,1)} %get-tuple-element.237, bf16[16,32,8,128]{3,2,1,0:T(8,128)(2,1)S(1)} %fusion.46), kind=kOutput, calls=%fused_computation.8.clone.1 | convolution fusion | flops 136310784 | bytes 6324224 | tf_op jit(solution)/shard_map/while/body/chn,khn->hck/dot_general | solution.py:32
  178.6 1.7 convolution_convert_fusion.3
  180.3 1.6 copy.55
  181.9 3.5 %bitcast_add_fusion.3 = f32[128,32,128]{0,2,1:T(8,128)} fusion(f32[128,32,128]{0,2,1:T(8,128)} %get-tuple-element.213, bf16[128,32,128]{0,2,1:T(8,128)(2,1)S(1)} %bitcast.92, f32[32,128,128]{1,2,0:T(8,128)S(1)} %get-tuple-element.191, f32[128,32]{0,1:T(8,128)S(1)} %get-tuple-element.192, f32[32,128]{1,0:T(8,128)S(1)} %get-tuple-element.228, ...), kind=kOutput, calls=%fused_computation.4.clone.1 | convolution fusion | flops 136839168 | bytes 7389184 | tf_op jit(solution)/shard_map/while/body/hck,khv->chv/dot_general | solution.py:47
  185.9 1.7 gather_fusion
  187.7 0.6 gather_fusion.1
  188.8 2.9 %fusion.46 = bf16[16,32,8,128]{3,2,1,0:T(8,128)(2,1)S(1)} fusion(bf16[128,512]{1,0:T(8,128)(2,1)S(1)} %fusion.45, bf16[512,4096]{1,0:T(8,128)(2,1)} %get-tuple-element.236), kind=kOutput, calls=%fused_computation.11.clone.1 | convolution fusion | flops 537395200 | bytes 5373952 | tf_op jit(solution)/shard_map/while/body/dot_general | solution.py:27
  191.7 3.3 %copy.53 = bf16[128,32,192]{0,2,1:T(8,128)(2,1)S(1)} copy(bf16[128,32,192]{2,0,1:T(8,128)(2,1)} %get-tuple-element.237) | data formatting | bytes 3145728 | tf_op jit(solution)/shard_map
  195.0 1.7 fusion.44
  196.8 2.9 %select_reduce_fusion.2 = (f32[32,128]{1,0:T(8,128)S(1)}, f32[32,128,128]{1,2,0:T(8,128)S(1)}) fusion(pred[128,128]{0,1:T(8,128)(4,1)S(1)} %broadcast_compare_fusion.2, f32[128,128,32]{1,0,2:T(8,128)} %fusion.44, bf16[128,32,192]{2,0,1:T(8,128)(2,1)} %get-tuple-element.237, bf16[16,32,8,128]{3,2,1,0:T(8,128)(2,1)S(1)} %fusion.46), kind=kOutput, calls=%fused_computation.8.clone.1 | convolution fusion | flops 136310784 | bytes 6324224 | tf_op jit(solution)/shard_map/while/body/chn,khn->hck/dot_general | solution.py:32
  199.9 1.7 convolution_convert_fusion.3
  201.6 1.6 copy.55
  203.2 3.5 %bitcast_add_fusion.3 = f32[128,32,128]{0,2,1:T(8,128)} fusion(f32[128,32,128]{0,2,1:T(8,128)} %get-tuple-element.213, bf16[128,32,128]{0,2,1:T(8,128)(2,1)S(1)} %bitcast.92, f32[32,128,128]{1,2,0:T(8,128)S(1)} %get-tuple-element.191, f32[128,32]{0,1:T(8,128)S(1)} %get-tuple-element.192, f32[32,128]{1,0:T(8,128)S(1)} %get-tuple-element.228, ...), kind=kOutput, calls=%fused_computation.4.clone.1 | convolution fusion | flops 136839168 | bytes 7389184 | tf_op jit(solution)/shard_map/while/body/hck,khv->chv/dot_general | solution.py:47
  207.3 1.7 gather_fusion
  209.1 0.6 gather_fusion.1
  210.1 2.9 %fusion.46 = bf16[16,32,8,128]{3,2,1,0:T(8,128)(2,1)S(1)} fusion(bf16[128,512]{1,0:T(8,128)(2,1)S(1)} %fusion.45, bf16[512,4096]{1,0:T(8,128)(2,1)} %get-tuple-element.236), kind=kOutput, calls=%fused_computation.11.clone.1 | convolution fusion | flops 537395200 | bytes 5373952 | tf_op jit(solution)/shard_map/while/body/dot_general | solution.py:27
  213.1 3.3 %copy.53 = bf16[128,32,192]{0,2,1:T(8,128)(2,1)S(1)} copy(bf16[128,32,192]{2,0,1:T(8,128)(2,1)} %get-tuple-element.237) | data formatting | bytes 3145728 | tf_op jit(solution)/shard_map
  216.4 1.7 fusion.44
  218.2 2.9 %select_reduce_fusion.2 = (f32[32,128]{1,0:T(8,128)S(1)}, f32[32,128,128]{1,2,0:T(8,128)S(1)}) fusion(pred[128,128]{0,1:T(8,128)(4,1)S(1)} %broadcast_compare_fusion.2, f32[128,128,32]{1,0,2:T(8,128)} %fusion.44, bf16[128,32,192]{2,0,1:T(8,128)(2,1)} %get-tuple-element.237, bf16[16,32,8,128]{3,2,1,0:T(8,128)(2,1)S(1)} %fusion.46), kind=kOutput, calls=%fused_computation.8.clone.1 | convolution fusion | flops 136310784 | bytes 6324224 | tf_op jit(solution)/shard_map/while/body/chn,khn->hck/dot_general | solution.py:32
  221.3 1.7 convolution_convert_fusion.3
  223.0 1.6 copy.55
  224.6 3.5 %bitcast_add_fusion.3 = f32[128,32,128]{0,2,1:T(8,128)} fusion(f32[128,32,128]{0,2,1:T(8,128)} %get-tuple-element.213, bf16[128,32,128]{0,2,1:T(8,128)(2,1)S(1)} %bitcast.92, f32[32,128,128]{1,2,0:T(8,128)S(1)} %get-tuple-element.191, f32[128,32]{0,1:T(8,128)S(1)} %get-tuple-element.192, f32[32,128]{1,0:T(8,128)S(1)} %get-tuple-element.228, ...), kind=kOutput, calls=%fused_computation.4.clone.1 | convolution fusion | flops 136839168 | bytes 7389184 | tf_op jit(solution)/shard_map/while/body/hck,khv->chv/dot_general | solution.py:47
  228.7 1.7 gather_fusion
  231.5 2.9 %fusion.46 = bf16[16,32,8,128]{3,2,1,0:T(8,128)(2,1)S(1)} fusion(bf16[128,512]{1,0:T(8,128)(2,1)S(1)} %fusion.45, bf16[512,4096]{1,0:T(8,128)(2,1)} %get-tuple-element.236), kind=kOutput, calls=%fused_computation.11.clone.1 | convolution fusion | flops 537395200 | bytes 5373952 | tf_op jit(solution)/shard_map/while/body/dot_general | solution.py:27
  234.4 3.3 %copy.53 = bf16[128,32,192]{0,2,1:T(8,128)(2,1)S(1)} copy(bf16[128,32,192]{2,0,1:T(8,128)(2,1)} %get-tuple-element.237) | data formatting | bytes 3145728 | tf_op jit(solution)/shard_map
  237.7 1.7 fusion.44
  239.6 2.9 %select_reduce_fusion.2 = (f32[32,128]{1,0:T(8,128)S(1)}, f32[32,128,128]{1,2,0:T(8,128)S(1)}) fusion(pred[128,128]{0,1:T(8,128)(4,1)S(1)} %broadcast_compare_fusion.2, f32[128,128,32]{1,0,2:T(8,128)} %fusion.44, bf16[128,32,192]{2,0,1:T(8,128)(2,1)} %get-tuple-element.237, bf16[16,32,8,128]{3,2,1,0:T(8,128)(2,1)S(1)} %fusion.46), kind=kOutput, calls=%fused_computation.8.clone.1 | convolution fusion | flops 136310784 | bytes 6324224 | tf_op jit(solution)/shard_map/while/body/chn,khn->hck/dot_general | solution.py:32
  242.7 1.7 convolution_convert_fusion.3
  244.4 1.6 copy.55
  246.0 3.5 %bitcast_add_fusion.3 = f32[128,32,128]{0,2,1:T(8,128)} fusion(f32[128,32,128]{0,2,1:T(8,128)} %get-tuple-element.213, bf16[128,32,128]{0,2,1:T(8,128)(2,1)S(1)} %bitcast.92, f32[32,128,128]{1,2,0:T(8,128)S(1)} %get-tuple-element.191, f32[128,32]{0,1:T(8,128)S(1)} %get-tuple-element.192, f32[32,128]{1,0:T(8,128)S(1)} %get-tuple-element.228, ...), kind=kOutput, calls=%fused_computation.4.clone.1 | convolution fusion | flops 136839168 | bytes 7389184 | tf_op jit(solution)/shard_map/while/body/hck,khv->chv/dot_general | solution.py:47
  249.9 2.4 copy.27
  252.4 1.5 fusion.16
  (92 shorter events, 6.0 us)
Async XLA Ops:
  6.5 74.3 %all-gather.5.cloned.1.call-start = ((), (), s32[]{:S(2)}) async-start(), calls=%async_computation.1 | async-start | bytes 4718592 | tf_op jit(solution)/shard_map/all_gather | solution.py:83
  7.3 5.3 %copy-start.4 = (bf16[1,4,4,64]{3,2,1,0:T(4,128)(2,1)S(1)}, bf16[1,4,4,64]{3,2,1,0:T(4,128)(2,1)}, u32[]{:S(2)}) copy-start(bf16[1,4,4,64]{3,2,1,0:T(4,128)(2,1)} %param.11) | copy-start | bytes 6148
  7.3 7.1 %copy-start.2 = (bf16[1,4,64,576]{3,2,1,0:T(8,128)(2,1)S(1)}, bf16[1,4,64,576]{3,2,1,0:T(8,128)(2,1)}, u32[]{:S(2)}) copy-start(bf16[1,4,64,576]{3,2,1,0:T(8,128)(2,1)} %param.10) | copy-start | bytes 884740
  7.3 147.1 %all-gather.3.cloned.1.call-start = ((), (), s32[]{:S(2)}) async-start(), calls=%async_computation | async-start | bytes 4718592 | tf_op jit(solution)/shard_map/all_gather | solution.py:82
  162.6 1.6 copy-start.3
  166.3 4.0 %copy-start.1 = (bf16[2,64,576]{2,1,0:T(8,128)(2,1)}, bf16[2,64,576]{2,1,0:T(8,128)(2,1)S(1)}, u32[]{:S(2)}) copy-start(bf16[2,64,576]{2,1,0:T(8,128)(2,1)S(1)} %broadcast_select_fusion.2) | copy-start | bytes 442372 | tf_op jit(solution)/shard_map/while
  170.3 3.3 %slice-start = ((bf16[2,64,576]{2,1,0:T(8,128)(2,1)}), bf16[2,64,64]{2,1,0:T(8,128)(2,1)S(1)}, s32[]{:S(2)}) async-start(bf16[2,64,576]{2,1,0:T(8,128)(2,1)} %copy-done.1), calls=%async_computation.2 | async-start | bytes 65536 | tf_op jit(solution)/shard_map/while/body/slice | solution.py:26
  175.4 3.1 %copy-start = (bf16[512,4096]{1,0:T(8,128)(2,1)S(1)}, bf16[512,4096]{1,0:T(8,128)(2,1)}, u32[]{:S(2)}) copy-start(bf16[512,4096]{1,0:T(8,128)(2,1)} %get-tuple-element.238) | copy-start | bytes 12582916 | tf_op jit(solution)/shard_map/while
  187.7 4.0 %copy-start.1 = (bf16[2,64,576]{2,1,0:T(8,128)(2,1)}, bf16[2,64,576]{2,1,0:T(8,128)(2,1)S(1)}, u32[]{:S(2)}) copy-start(bf16[2,64,576]{2,1,0:T(8,128)(2,1)S(1)} %broadcast_select_fusion.2) | copy-start | bytes 442372 | tf_op jit(solution)/shard_map/while
  191.7 3.3 %slice-start = ((bf16[2,64,576]{2,1,0:T(8,128)(2,1)}), bf16[2,64,64]{2,1,0:T(8,128)(2,1)S(1)}, s32[]{:S(2)}) async-start(bf16[2,64,576]{2,1,0:T(8,128)(2,1)} %copy-done.1), calls=%async_computation.2 | async-start | bytes 65536 | tf_op jit(solution)/shard_map/while/body/slice | solution.py:26
  196.8 3.1 %copy-start = (bf16[512,4096]{1,0:T(8,128)(2,1)S(1)}, bf16[512,4096]{1,0:T(8,128)(2,1)}, u32[]{:S(2)}) copy-start(bf16[512,4096]{1,0:T(8,128)(2,1)} %get-tuple-element.238) | copy-start | bytes 12582916 | tf_op jit(solution)/shard_map/while
  209.1 4.0 %copy-start.1 = (bf16[2,64,576]{2,1,0:T(8,128)(2,1)}, bf16[2,64,576]{2,1,0:T(8,128)(2,1)S(1)}, u32[]{:S(2)}) copy-start(bf16[2,64,576]{2,1,0:T(8,128)(2,1)S(1)} %broadcast_select_fusion.2) | copy-start | bytes 442372 | tf_op jit(solution)/shard_map/while
  213.1 3.3 %slice-start = ((bf16[2,64,576]{2,1,0:T(8,128)(2,1)}), bf16[2,64,64]{2,1,0:T(8,128)(2,1)S(1)}, s32[]{:S(2)}) async-start(bf16[2,64,576]{2,1,0:T(8,128)(2,1)} %copy-done.1), calls=%async_computation.2 | async-start | bytes 65536 | tf_op jit(solution)/shard_map/while/body/slice | solution.py:26
  218.2 3.1 %copy-start = (bf16[512,4096]{1,0:T(8,128)(2,1)S(1)}, bf16[512,4096]{1,0:T(8,128)(2,1)}, u32[]{:S(2)}) copy-start(bf16[512,4096]{1,0:T(8,128)(2,1)} %get-tuple-element.238) | copy-start | bytes 12582916 | tf_op jit(solution)/shard_map/while
  230.4 4.0 %copy-start.1 = (bf16[2,64,576]{2,1,0:T(8,128)(2,1)}, bf16[2,64,576]{2,1,0:T(8,128)(2,1)S(1)}, u32[]{:S(2)}) copy-start(bf16[2,64,576]{2,1,0:T(8,128)(2,1)S(1)} %broadcast_select_fusion.2) | copy-start | bytes 442372 | tf_op jit(solution)/shard_map/while
  234.4 3.3 %slice-start = ((bf16[2,64,576]{2,1,0:T(8,128)(2,1)}), bf16[2,64,64]{2,1,0:T(8,128)(2,1)S(1)}, s32[]{:S(2)}) async-start(bf16[2,64,576]{2,1,0:T(8,128)(2,1)} %copy-done.1), calls=%async_computation.2 | async-start | bytes 65536 | tf_op jit(solution)/shard_map/while/body/slice | solution.py:26
  239.5 3.1 %copy-start = (bf16[512,4096]{1,0:T(8,128)(2,1)S(1)}, bf16[512,4096]{1,0:T(8,128)(2,1)}, u32[]{:S(2)}) copy-start(bf16[512,4096]{1,0:T(8,128)(2,1)} %get-tuple-element.238) | copy-start | bytes 12582916 | tf_op jit(solution)/shard_map/while
Sparse Core Ops, SparseCore 0:
  9.5 71.3 all-gather.4
  83.0 71.3 all-gather.2
where the time goes:
time: 265 us; the launch traced here: 261 us
  waiting for transfers between devices  131 us (49%)
  local copies, waits for them, and re-layouts  55.1 us (21%)
  matrix products  51.1 us (19%)
  between operations  14.1 us (5%)
  other arithmetic  4.73 us (2%)
  blocking collectives  4.21 us (2%)
    all_gather x1, waiting for transfers between devices, on_device(): lax.all_gather(w_keys, 'ctx', axis=0, tiled=True)  65.2 us
    all_gather x1, waiting for transfers between devices, on_device(): lax.all_gather(w_values, 'ctx', axis=0, tiled=True)  64.1 us
    unnamed x9, local copies, waits for them, and re-layouts  20.5 us
    dot_general x4, matrix products, attend_block(): jnp.einsum('hck,khv->chv', weights, value_rows, preferred_element_type=jn...  14 us
    another operation x4, local copies, waits for them, and re-layouts  13.1 us
    dot_general x4, matrix products, attend_block(): jnp.einsum('chn,khn->hck', span_query[:, :, :nope_width], key_nope, prefe...  11.7 us
    dot_general x4, matrix products, attend_block(): jnp.dot(latent, up_keys, preferred_element_type=jnp.float32)  11.7 us
    dot_general x4, matrix products, attend_block(): jnp.einsum('chr,kr->hck', span_query[:, :, nope_width:], rotary, preferre...  6.93 us
  transfers between devices with their start and end apart: 2, of which 2 were waited for; matrix products, arithmetic and copies ran while one was open for 5% of the time, Pallas kernels for 0%

commit v1 on v0

--- a/solution.py
+++ b/solution.py
@@ -1,11 +1,17 @@
+import functools
 import math
 
 import jax
 import jax.numpy as jnp
 from jax import lax
+from jax.experimental import pallas as pl
+from jax.experimental.pallas import tpu as pltpu
 from jax.sharding import PartitionSpec as P
 
 NEGATIVE = -1e30
+MESH = pl.DeviceIdType.MESH
+PAIR = 2
+LAG = 2
 
 
 def attend_block(
@@ -108,9 +114,236 @@
     return finish(row_total, summed)
 
 
+def gather_attend(
+    shard_columns, q_in, k_in, t_in, w_in, out, q_rx, k_all, t_rx, w_all, rot, stage,
+    own_sem, core_send, core_recv, relay_send, relay_recv, k_send, k_recv, t_send, t_recv,
+    q_send, q_recv, z_send, z_recv, x_send, x_recv, f_send, f_recv, o_send, o_recv
+):
+    chunk_count = w_in.shape[1]
+    latent_width = w_all.shape[2] * w_all.shape[3]
+    nope = q_in.shape[-1]
+    span = q_in.shape[-2]
+    rope = nope // PAIR
+    key_count = k_all.shape[1] * k_all.shape[2]
+    scale = 1.0 / math.sqrt(nope + rope)
+    y, ctx, core = lax.axis_index("groups"), lax.axis_index("ctx"), lax.axis_index("head")
+    row, side = ctx // 2, lax.rem(ctx, 2)
+    y_peer = {"groups": 1 - y}
+    core_peer = {"head": 1 - core}
+    x_peer = {"ctx": 2 * row + 1 - side}
+
+    def z_index(offset):
+        return 2 * lax.rem(row + offset, shard_columns) + side
+
+    barrier = pltpu.get_barrier_semaphore()
+    peers = [y_peer, core_peer, x_peer] + [{"ctx": z_index(d)} for d in range(1, shard_columns)]
+    for peer in peers:
+        pl.semaphore_signal(barrier, inc=1, device_id=peer, device_id_type=MESH)
+    pl.semaphore_wait(barrier, len(peers))
+
+    def remote(source, target, send, recv, peer):
+        return pltpu.make_async_remote_copy(
+            src_ref=source, dst_ref=target, send_sem=send, recv_sem=recv,
+            device_id=peer, device_id_type=MESH,
+        )
+
+    k_copy = remote(k_in, k_all.at[y, core], k_send, k_recv, y_peer)
+    t_copy = remote(t_in, t_rx, t_send, t_recv, y_peer)
+    core_copy = remote(k_in, k_all.at[y, core], core_send, core_recv, core_peer)
+    relay_copy = remote(
+        k_all.at[1 - y, core], k_all.at[1 - y, core], relay_send, relay_recv, core_peer
+    )
+    k_own = pltpu.make_async_copy(k_in, k_all.at[y, core], own_sem.at[0])
+    w_own = pltpu.make_async_copy(w_in.at[y], w_all.at[:, :, ctx], own_sem.at[1])
+
+    def q_copy(c):
+        return remote(q_in.at[1 - y, c], q_rx.at[c], q_send.at[c], q_recv.at[c], y_peer)
+
+    def z_copy(c, d):
+        return remote(
+            w_in.at[y, c], w_all.at[c, :, ctx], z_send.at[c, d - 1], z_recv.at[c, d - 1],
+            {"ctx": z_index(d)},
+        )
+
+    def x_copy(c):
+        return remote(w_in.at[y, c], w_all.at[c, :, ctx], x_send.at[c], x_recv.at[c], x_peer)
+
+    def f_copy(c, d):
+        block = w_all.at[c, :, z_index(shard_columns - d)]
+        return remote(block, block, f_send.at[c, d - 1], f_recv.at[c, d - 1], x_peer)
+
+    def o_copy(c):
+        return remote(stage.at[c], out.at[y, c], o_send.at[c], o_recv.at[c], y_peer)
+
+    k_copy.start()
+    t_copy.start()
+    core_copy.start()
+    k_own.start()
+    w_own.start()
+
+    def begin(c, carry):
+        for d in range(1, shard_columns):
+            z_copy(c, d).start()
+        x_copy(c).start()
+        q_copy(c).start()
+        return carry
+
+    lax.fori_loop(0, chunk_count, begin, 0)
+    k_own.wait()
+    w_own.wait()
+    k_copy.wait_recv()
+    relay_copy.start()
+    t_copy.wait_recv()
+    core_copy.wait_recv()
+    relay_copy.wait_recv()
+    lane = lax.broadcasted_iota(jnp.int32, (key_count, nope), 1)
+    for r in range(2):
+        both = k_all[r, :, :, latent_width:].reshape(key_count, nope)
+        rot[r, 0] = jnp.where(lane < rope, both, jnp.zeros_like(both))
+        rot[r, 1] = jnp.where(lane < rope, jnp.zeros_like(both), both)
+    row_position = lax.broadcasted_iota(jnp.int32, (span, key_count), 0)
+
+    def attend(c, request, q_ref, t_ref, put):
+        latent = k_all[request, :, :, :latent_width].reshape(key_count, latent_width)
+        visible = t_ref[0:1, :] <= row_position
+        for h in range(PAIR):
+            weight = w_all[c, h].reshape(latent_width, -1)
+            up = jnp.dot(latent, weight, preferred_element_type=jnp.float32).astype(jnp.bfloat16)
+            keys = jnp.concatenate([up[:, :nope], rot[request, h]], axis=1)
+            query = jnp.concatenate([q_ref[h], q_ref[PAIR]], axis=1)
+            scores = lax.dot_general(
+                query, keys, (((1,), (1,)), ((), ())), preferred_element_type=jnp.float32
+            )
+            scores = jnp.where(visible, scores * scale, NEGATIVE)
+            top = jnp.max(scores, axis=1, keepdims=True)
+            raw = jnp.where(visible, jnp.exp(scores - top), 0.0)
+            total = jnp.sum(raw, axis=1, keepdims=True)
+            summed = jnp.dot(
+                raw.astype(jnp.bfloat16), up[:, nope:], preferred_element_type=jnp.float32
+            )
+            put(h, (summed / total).astype(jnp.bfloat16))
+
+    def advance(c, carry):
+        @pl.when(c < chunk_count)
+        def _():
+            for d in range(1, shard_columns):
+                z_copy(c, d).wait_recv()
+                f_copy(c, d).start()
+
+        @pl.when(c >= LAG)
+        def _():
+            b = c - LAG
+            x_copy(b).wait_recv()
+            for d in range(1, shard_columns):
+                f_copy(b, d).wait_recv()
+            q_copy(b).wait_recv()
+
+            def put_stage(h, value):
+                stage[b, h] = value
+
+            def put_out(h, value):
+                out[y, b, h] = value
+
+            attend(b, 1 - y, q_rx.at[b], t_rx, put_stage)
+            attend(b, y, q_in.at[y, b], t_in, put_out)
+            o_copy(b).start()
+
+        return carry
+
+    lax.fori_loop(0, chunk_count + LAG, advance, 0)
+    k_copy.wait_send()
+    t_copy.wait_send()
+    core_copy.wait_send()
+    relay_copy.wait_send()
+
+    def end(c, carry):
+        q_copy(c).wait_send()
+        x_copy(c).wait_send()
+        for d in range(1, shard_columns):
+            z_copy(c, d).wait_send()
+            f_copy(c, d).wait_send()
+        o_copy(c).wait()
+        return carry
+
+    lax.fori_loop(0, chunk_count, end, 0)
+
+
+def shared_on_device(
+    shards, queries, latent_pages, page_scales, page_table, lengths, w_keys, w_values
+):
+    _, span, heads, _ = queries.shape
+    latent_rows, _, nope = w_keys.shape
+    _, slots, page, width = latent_pages.shape
+    latent_width = latent_rows * shards
+    rope = width - latent_width
+    groups = page_scales.shape[2]
+    chunks = heads // (2 * PAIR)
+    keys = slots * page
+    columns = shards // 2
+    w_in = jnp.concatenate([jnp.swapaxes(w_keys, 0, 1), jnp.swapaxes(w_values, 0, 1)], axis=-1)
+    w_in = w_in.reshape(2, chunks, PAIR, latent_rows, 2 * nope)
+    query = queries[0]
+    q_nope = jnp.swapaxes(query[:, :, :nope], 0, 1).reshape(2, chunks, PAIR, span, nope)
+    q_rope = query[:, :, nope:].reshape(span, heads // PAIR, nope)
+    q_rope = jnp.swapaxes(q_rope, 0, 1).reshape(2, chunks, 1, span, nope)
+    q_in = jnp.concatenate([q_nope, q_rope], axis=2)
+    codes = latent_pages[0, :, :, :latent_width].astype(jnp.float32)
+    codes = codes.reshape(slots, page, groups, latent_width // groups)
+    factor = jnp.swapaxes(page_scales[0], 1, 2).astype(jnp.float32)[..., None]
+    latent = (codes * factor).reshape(keys, latent_width).astype(jnp.bfloat16)
+    rotary = latent_pages[0, :, :, latent_width:].reshape(keys, rope)
+    k_in = jnp.concatenate([latent, rotary, rotary], axis=1)
+    pool = page_table.shape[1]
+    places = jnp.arange(pool, dtype=jnp.int32)
+    order = jnp.sum(jnp.where(page_table[0][:, None] == places[None], places[:, None], 0), axis=0)
+    first = order[:, None] * page + jnp.arange(page, dtype=jnp.int32)[None]
+    first = first.reshape(1, pool * page) - (lengths[0] - span)
+    t_in = jnp.broadcast_to(first, (8, pool * page))
+    dma, vmem = pltpu.SemaphoreType.DMA, pltpu.VMEM
+    bf16 = jnp.bfloat16
+    out = pl.pallas_call(
+        functools.partial(gather_attend, columns),
+        out_shape=jax.ShapeDtypeStruct((2, chunks, PAIR, span, nope), bf16),
+        in_specs=[pl.BlockSpec(memory_space=vmem)] * 4,
+        out_specs=pl.BlockSpec(memory_space=vmem),
+        scratch_shapes=[
+            vmem((chunks, PAIR + 1, span, nope), bf16),
+            vmem((2, 2, keys, k_in.shape[1]), bf16),
+            vmem(t_in.shape, jnp.int32),
+            vmem((chunks, PAIR, shards, latent_rows, 2 * nope), bf16),
+            vmem((2, 2, 2 * keys, nope), bf16),
+            vmem((chunks, PAIR, span, nope), bf16),
+            dma((2,)), dma, dma, dma, dma, dma, dma, dma, dma,
+            dma((chunks,)), dma((chunks,)),
+            dma((chunks, columns - 1)), dma((chunks, columns - 1)),
+            dma((chunks,)), dma((chunks,)),
+            dma((chunks, columns - 1)), dma((chunks, columns - 1)),
+            dma((chunks,)), dma((chunks,)),
+        ],
+        compiler_params=pltpu.CompilerParams(
+            collective_id=0, has_side_effects=True, vmem_limit_bytes=48 * 1024 * 1024
+        ),
+    )(q_in, k_in, t_in, w_in)
+    return jnp.swapaxes(out.reshape(heads, span, nope), 0, 1)[None]
+
+
+def body_for(mesh, queries, latent_pages, page_scales, page_table, lengths, w_keys, w_values):
+    args = (queries, latent_pages, page_scales, page_table, lengths, w_keys, w_values)
+    shards = mesh.shape["ctx"]
+    rope = latent_pages.shape[3] - w_keys.shape[0] * shards
+    fits = (
+        mesh.shape["groups"] == 2 and mesh.shape["head"] == 2 and shards % 2 == 0
+        and shards >= 4 and w_keys.shape[0] % 16 == 0 and queries.shape[2] % (2 * PAIR) == 0
+        and w_keys.shape == w_values.shape and 2 * rope == w_keys.shape[2]
+    )
+    if fits:
+        return shared_on_device(shards, *args)
+    return on_device(*args)
+
+
 def solution(mesh):
     return jax.shard_map(
-        on_device,
+        functools.partial(body_for, mesh),
         mesh=mesh,
         in_specs=(
             P(("groups", "ctx"), None, "head", None),

time: 265 us -> 77.8 us (0.29)
  the two profiles are of different devices: /device:TPU:26 before, /device:TPU:0 now
where the time goes in v1:
time: 77.8 us; the launch traced here: 77.5 us
  Pallas kernels  67.6 us (87%)
  local copies, waits for them, and re-layouts  7.15 us (9%)
  other arithmetic  1.99 us (3%)
  between operations  0.81 us (1%)
    pallas_call x1, Pallas kernels, shared_on_device(): pl.pallas_call(functools.partial(gather_attend, columns), out_shape=jax.S...  67.6 us
    transpose x2, local copies, waits for them, and re-layouts, shared_on_device(): jnp.swapaxes(query[:, :, :nope], 0, 1).reshape(2, chunks, PAIR, span, nope)  1.97 us
    reshape x1, local copies, waits for them, and re-layouts, shared_on_device(): return jnp.swapaxes(out.reshape(heads, span, nope), 0, 1)[None]  1.65 us

profile of v1, /device:TPU:0, one launch (start us, length us, event | category | flops | bytes accessed | tf_op | source)
XLA Modules:
  0.0 77.5 jit_solution(17406868783531589607)
XLA Ops:
  0.0 0.0 slice-start.1
  0.0 0.0 slice-start
  0.7 0.7 select_reduce_fusion
  1.5 0.1 add_subtract_fusion
  1.5 0.1 sub.23
  1.6 0.7 convert_bitcast_fusion
  2.3 0.1 copy.15
  2.4 0.3 mul.19
  2.8 0.0 slice-done.1
  2.8 0.1 fusion
  2.9 0.0 slice-done
  2.9 0.1 pad_maximum_fusion.2.k_in
  3.0 1.1 %slice.17 = bf16[128,32,64]{0,2,1:T(8,128)(2,1)S(1)} slice(bf16[128,32,192]{0,2,1:T(8,128)(2,1)} %bitcast.40), slice={[0:128], [0:32], [128:192]} | slice | bytes 1048576 | tf_op jit(solution)/shard_map/slice | solution.py:287
  4.1 0.3 copy.14
  4.4 1.3 %slice_bitcast_fusion = bf16[32,128,128]{1,2,0:T(8,128)(2,1)S(1)} fusion(bf16[128,32,192]{0,2,1:T(8,128)(2,1)} %bitcast.41), kind=kLoop, calls=%fused_computation.1 | loop fusion | bytes 2097152 | tf_op jit(solution)/shard_map/transpose | solution.py:286
  5.7 0.7 copy.13
  6.3 0.0 copy-start
  6.3 0.0 copy-start.1
  6.4 0.1 pad_maximum_fusion.q_in
  6.5 0.9 %copy-done = bf16[64,32,128]{2,1,0:T(8,128)(2,1)S(1)} copy-done((bf16[64,32,128]{2,1,0:T(8,128)(2,1)S(1)}, bf16[64,32,128]{2,1,0:T(8,128)(2,1)}, u32[]{:S(2)}) %copy-start) | copy-done | bytes 524312
  7.4 0.2 copy-done.1
  7.5 0.1 pad_maximum_fusion.1
  7.7 0.6 copy.16
  8.3 67.6 %shard_map.73 = bf16[2,8,2,128,128]{4,3,2,1,0:T(8,128)(2,1)S(1)} custom-call(bf16[2,8,3,128,128]{4,3,2,1,0:T(8,128)(2,1)S(1)} %pad_maximum_fusion.q_in, bf16[256,640]{1,0:T(8,128)(2,1)S(1)} %pad_maximum_fusion.2.k_in, s32[8,512]{1,0:T(8,128)S(1)} %broadcast_in_dim.27.t_in, bf16[2,8,2,64,256]{4,3,2,1,0:T(8,128)(2,1)S(1)} %bitcast.34), custom_call_target="tpu_custom_call" | custom-call | tf_op jit(solution)/shard_map/pallas_call | solution.py:304
  75.9 1.6 %copy.21 = bf16[32,128,128]{2,0,1:T(8,128)(2,1)} copy(bf16[32,128,128]{2,1,0:T(8,128)(2,1)S(1)} %bitcast.35) | data formatting | bytes 2097152 | tf_op jit(solution)/shard_map/reshape | solution.py:327
  (2 shorter events, 0.0 us)
Async XLA Ops:
  0.0 2.8 %slice-start.1 = ((bf16[1,4,64,576]{3,2,1,0:T(8,128)(2,1)}), bf16[1,4,64,512]{3,2,1,0:T(8,128)(2,1)S(1)}, s32[]{:S(2)}) async-start(bf16[1,4,64,576]{3,2,1,0:T(8,128)(2,1)} %param.8), calls=%async_computation.1 | async-start | bytes 524288 | tf_op jit(solution)/shard_map/slice | solution.py:290
  0.0 2.9 %slice-start = ((bf16[1,4,64,576]{3,2,1,0:T(8,128)(2,1)}), bf16[1,4,64,64]{3,2,1,0:T(8,128)(2,1)S(1)}, s32[]{:S(2)}) async-start(bf16[1,4,64,576]{3,2,1,0:T(8,128)(2,1)} %param.8), calls=%async_computation | async-start | bytes 131072 | tf_op jit(solution)/shard_map/slice | solution.py:294
  6.3 1.0 %copy-start = (bf16[64,32,128]{2,1,0:T(8,128)(2,1)S(1)}, bf16[64,32,128]{2,1,0:T(8,128)(2,1)}, u32[]{:S(2)}) copy-start(bf16[64,32,128]{2,1,0:T(8,128)(2,1)} %param.13) | copy-start | bytes 1572868
  6.3 1.2 %copy-start.1 = (bf16[64,32,128]{2,1,0:T(8,128)(2,1)S(1)}, bf16[64,32,128]{2,1,0:T(8,128)(2,1)}, u32[]{:S(2)}) copy-start(bf16[64,32,128]{2,1,0:T(8,128)(2,1)} %param.12) | copy-start | bytes 1572868

commit v2 on v1

--- a/solution.py
+++ b/solution.py
@@ -11,7 +11,7 @@
 NEGATIVE = -1e30
 MESH = pl.DeviceIdType.MESH
 PAIR = 2
-LAG = 2
+LAG = 1
 
 
 def attend_block(
@@ -115,15 +115,16 @@
 
 
 def gather_attend(
-    shard_columns, q_in, k_in, t_in, w_in, out, q_rx, k_all, t_rx, w_all, rot, stage,
+    shard_columns, q_in, k_in, t_in, w_in, out, q_rx, q_own, k_all, t_rx, w_all, rot, late, stage,
     own_sem, core_send, core_recv, relay_send, relay_recv, k_send, k_recv, t_send, t_recv,
-    q_send, q_recv, z_send, z_recv, x_send, x_recv, f_send, f_recv, o_send, o_recv
+    q_send, q_recv, z_send, z_recv, x_send, x_recv, f_send, f_recv,
+    r_send, g_send, o_send, o_recv
 ):
     chunk_count = w_in.shape[1]
     latent_width = w_all.shape[2] * w_all.shape[3]
-    nope = q_in.shape[-1]
-    span = q_in.shape[-2]
-    rope = nope // PAIR
+    span = q_in.shape[-1]
+    nope = w_all.shape[-1] // 2
+    rope = q_in.shape[-2] - nope
     key_count = k_all.shape[1] * k_all.shape[2]
     scale = 1.0 / math.sqrt(nope + rope)
     y, ctx, core = lax.axis_index("groups"), lax.axis_index("ctx"), lax.axis_index("head")
@@ -156,21 +157,61 @@
     k_own = pltpu.make_async_copy(k_in, k_all.at[y, core], own_sem.at[0])
     w_own = pltpu.make_async_copy(w_in.at[y], w_all.at[:, :, ctx], own_sem.at[1])
 
+    q_mine = pltpu.make_async_copy(q_in.at[y], q_own, own_sem.at[2])
+    last = shard_columns - 1
+    relays = jnp.logical_or(row == 1, row == last - 1)
+    relay_source = jnp.where(row == 1, last, 0)
+    partner = row + 1 - 2 * lax.rem(row, 2)
+
+    def far(other):
+        return jnp.abs(other - row) == last
+
+    def block(c, source_row, source_side):
+        return w_all.at[c, :, 2 * source_row + source_side]
+
     def q_copy(c):
         return remote(q_in.at[1 - y, c], q_rx.at[c], q_send.at[c], q_recv.at[c], y_peer)
 
     def z_copy(c, d):
         return remote(
-            w_in.at[y, c], w_all.at[c, :, ctx], z_send.at[c, d - 1], z_recv.at[c, d - 1],
+            w_in.at[y, c], block(c, row, side), z_send.at[c, d - 1], z_recv.at[c, row],
             {"ctx": z_index(d)},
         )
 
+    def z_arrival(c, source):
+        return remote(
+            w_in.at[y, c], block(c, source, side), z_send.at[c, 0], z_recv.at[c, source], x_peer
+        )
+
+    def r_copy(c):
+        moved = block(c, relay_source, side)
+        return remote(
+            moved, moved, r_send.at[c], z_recv.at[c, relay_source],
+            {"ctx": 2 * (last - relay_source) + side},
+        )
+
     def x_copy(c):
-        return remote(w_in.at[y, c], w_all.at[c, :, ctx], x_send.at[c], x_recv.at[c], x_peer)
-
-    def f_copy(c, d):
-        block = w_all.at[c, :, z_index(shard_columns - d)]
-        return remote(block, block, f_send.at[c, d - 1], f_recv.at[c, d - 1], x_peer)
+        return remote(w_in.at[y, c], block(c, row, side), x_send.at[c], x_recv.at[c], x_peer)
+
+    def x_arrival(c):
+        return remote(w_in.at[y, c], block(c, row, 1 - side), x_send.at[c], x_recv.at[c], x_peer)
+
+    def f_copy(c, source):
+        moved = block(c, source, side)
+        return remote(moved, moved, f_send.at[c, source], f_recv.at[c, source], x_peer)
+
+    def f_arrival(c, source):
+        moved = block(c, source, 1 - side)
+        return remote(moved, moved, f_send.at[c, source], f_recv.at[c, source], x_peer)
+
+    def g_copy(c):
+        moved = block(c, row, 1 - side)
+        return remote(
+            moved, moved, g_send.at[c], f_recv.at[c, row], {"ctx": 2 * partner + side}
+        )
+
+    def over_x(c, source):
+        return jnp.logical_or(lax.rem(c, 2) == 0, source != partner)
 
     def o_copy(c):
         return remote(stage.at[c], out.at[y, c], o_send.at[c], o_recv.at[c], y_peer)
@@ -179,11 +220,14 @@
     t_copy.start()
     core_copy.start()
     k_own.start()
+    q_mine.start()
     w_own.start()
 
     def begin(c, carry):
         for d in range(1, shard_columns):
-            z_copy(c, d).start()
+            @pl.when(jnp.logical_not(far(lax.rem(row + d, shard_columns))))
+            def _():
+                z_copy(c, d).start()
         x_copy(c).start()
         q_copy(c).start()
         return carry
@@ -191,51 +235,65 @@
     lax.fori_loop(0, chunk_count, begin, 0)
     k_own.wait()
     w_own.wait()
+    q_mine.wait()
     k_copy.wait_recv()
     relay_copy.start()
     t_copy.wait_recv()
     core_copy.wait_recv()
     relay_copy.wait_recv()
-    lane = lax.broadcasted_iota(jnp.int32, (key_count, nope), 1)
-    for r in range(2):
-        both = k_all[r, :, :, latent_width:].reshape(key_count, nope)
-        rot[r, 0] = jnp.where(lane < rope, both, jnp.zeros_like(both))
-        rot[r, 1] = jnp.where(lane < rope, jnp.zeros_like(both), both)
-    row_position = lax.broadcasted_iota(jnp.int32, (span, key_count), 0)
-
-    def attend(c, request, q_ref, t_ref, put):
+    page = key_count // t_in.shape[1]
+    offset = lax.broadcasted_iota(jnp.int32, (page, span), 0)
+    offset = offset - lax.broadcasted_iota(jnp.int32, (page, span), 1)
+    for request, t_ref in ((y, t_in), (1 - y, t_rx)):
+        rot[request] = k_all[request, :, :, latent_width:].reshape(key_count, rope)
+        late[request] = jnp.concatenate(
+            [t_ref[0:1, p : p + 1] + offset for p in range(t_in.shape[1])], axis=0
+        )
+
+    def attend(c, request, q_ref, put):
         latent = k_all[request, :, :, :latent_width].reshape(key_count, latent_width)
-        visible = t_ref[0:1, :] <= row_position
+        visible = late[request] <= 0
         for h in range(PAIR):
             weight = w_all[c, h].reshape(latent_width, -1)
             up = jnp.dot(latent, weight, preferred_element_type=jnp.float32).astype(jnp.bfloat16)
-            keys = jnp.concatenate([up[:, :nope], rot[request, h]], axis=1)
-            query = jnp.concatenate([q_ref[h], q_ref[PAIR]], axis=1)
-            scores = lax.dot_general(
-                query, keys, (((1,), (1,)), ((), ())), preferred_element_type=jnp.float32
+            keys = jnp.concatenate([up[:, :nope], rot[request]], axis=1)
+            scores = jnp.dot(keys, q_ref[h], preferred_element_type=jnp.float32)
+            scores = jnp.where(visible, scores * scale, NEGATIVE)
+            top = jnp.max(scores, axis=0, keepdims=True)
+            raw = jnp.where(visible, jnp.exp(scores - top), 0.0)
+            total = jnp.sum(raw, axis=0, keepdims=True)
+            summed = lax.dot_general(
+                up[:, nope:], raw.astype(jnp.bfloat16), (((0,), (0,)), ((), ())),
+                preferred_element_type=jnp.float32,
             )
-            scores = jnp.where(visible, scores * scale, NEGATIVE)
-            top = jnp.max(scores, axis=1, keepdims=True)
-            raw = jnp.where(visible, jnp.exp(scores - top), 0.0)
-            total = jnp.sum(raw, axis=1, keepdims=True)
-            summed = jnp.dot(
-                raw.astype(jnp.bfloat16), up[:, nope:], preferred_element_type=jnp.float32
-            )
-            put(h, (summed / total).astype(jnp.bfloat16))
+            put(h, jnp.transpose(summed / total).astype(jnp.bfloat16))
 
     def advance(c, carry):
         @pl.when(c < chunk_count)
         def _():
+            x_arrival(c).wait_recv()
+
+            @pl.when(lax.rem(c, 2) == 1)
+            def _():
+                g_copy(c).start()
+
             for d in range(1, shard_columns):
-                z_copy(c, d).wait_recv()
-                f_copy(c, d).start()
+                source = lax.rem(row + d, shard_columns)
+                z_arrival(c, source).wait_recv()
+
+                @pl.when(jnp.logical_and(relays, source == relay_source))
+                def _():
+                    r_copy(c).start()
+
+                @pl.when(over_x(c, source))
+                def _():
+                    f_copy(c, source).start()
 
         @pl.when(c >= LAG)
         def _():
             b = c - LAG
-            x_copy(b).wait_recv()
             for d in range(1, shard_columns):
-                f_copy(b, d).wait_recv()
+                f_arrival(b, lax.rem(row + d, shard_columns)).wait_recv()
             q_copy(b).wait_recv()
 
             def put_stage(h, value):
@@ -244,8 +302,8 @@
             def put_out(h, value):
                 out[y, b, h] = value
 
-            attend(b, 1 - y, q_rx.at[b], t_rx, put_stage)
-            attend(b, y, q_in.at[y, b], t_in, put_out)
+            attend(b, 1 - y, q_rx.at[b], put_stage)
+            attend(b, y, q_own.at[b], put_out)
             o_copy(b).start()
 
         return carry
@@ -260,8 +318,24 @@
         q_copy(c).wait_send()
         x_copy(c).wait_send()
         for d in range(1, shard_columns):
-            z_copy(c, d).wait_send()
-            f_copy(c, d).wait_send()
+            other = lax.rem(row + d, shard_columns)
+
+            @pl.when(jnp.logical_not(far(other)))
+            def _():
+                z_copy(c, d).wait_send()
+
+            @pl.when(over_x(c, other))
+            def _():
+                f_copy(c, other).wait_send()
+
+        @pl.when(relays)
+        def _():
+            r_copy(c).wait_send()
+
+        @pl.when(lax.rem(c, 2) == 1)
+        def _():
+            g_copy(c).wait_send()
+
         o_copy(c).wait()
         return carry
 
@@ -282,43 +356,39 @@
     columns = shards // 2
     w_in = jnp.concatenate([jnp.swapaxes(w_keys, 0, 1), jnp.swapaxes(w_values, 0, 1)], axis=-1)
     w_in = w_in.reshape(2, chunks, PAIR, latent_rows, 2 * nope)
-    query = queries[0]
-    q_nope = jnp.swapaxes(query[:, :, :nope], 0, 1).reshape(2, chunks, PAIR, span, nope)
-    q_rope = query[:, :, nope:].reshape(span, heads // PAIR, nope)
-    q_rope = jnp.swapaxes(q_rope, 0, 1).reshape(2, chunks, 1, span, nope)
-    q_in = jnp.concatenate([q_nope, q_rope], axis=2)
+    q_in = jnp.transpose(queries[0], (1, 2, 0)).reshape(2, chunks, PAIR, -1, span)
     codes = latent_pages[0, :, :, :latent_width].astype(jnp.float32)
     codes = codes.reshape(slots, page, groups, latent_width // groups)
     factor = jnp.swapaxes(page_scales[0], 1, 2).astype(jnp.float32)[..., None]
     latent = (codes * factor).reshape(keys, latent_width).astype(jnp.bfloat16)
     rotary = latent_pages[0, :, :, latent_width:].reshape(keys, rope)
-    k_in = jnp.concatenate([latent, rotary, rotary], axis=1)
+    k_in = jnp.concatenate([latent, rotary], axis=1)
     pool = page_table.shape[1]
     places = jnp.arange(pool, dtype=jnp.int32)
     order = jnp.sum(jnp.where(page_table[0][:, None] == places[None], places[:, None], 0), axis=0)
-    first = order[:, None] * page + jnp.arange(page, dtype=jnp.int32)[None]
-    first = first.reshape(1, pool * page) - (lengths[0] - span)
-    t_in = jnp.broadcast_to(first, (8, pool * page))
+    t_in = jnp.broadcast_to((order * page - (lengths[0] - span))[None], (8, pool))
     dma, vmem = pltpu.SemaphoreType.DMA, pltpu.VMEM
     bf16 = jnp.bfloat16
     out = pl.pallas_call(
         functools.partial(gather_attend, columns),
         out_shape=jax.ShapeDtypeStruct((2, chunks, PAIR, span, nope), bf16),
-        in_specs=[pl.BlockSpec(memory_space=vmem)] * 4,
+        in_specs=[pl.BlockSpec(memory_space=pl.ANY)] + [pl.BlockSpec(memory_space=vmem)] * 3,
         out_specs=pl.BlockSpec(memory_space=vmem),
         scratch_shapes=[
-            vmem((chunks, PAIR + 1, span, nope), bf16),
+            vmem(q_in.shape[1:], bf16),
+            vmem(q_in.shape[1:], bf16),
             vmem((2, 2, keys, k_in.shape[1]), bf16),
             vmem(t_in.shape, jnp.int32),
             vmem((chunks, PAIR, shards, latent_rows, 2 * nope), bf16),
-            vmem((2, 2, 2 * keys, nope), bf16),
+            vmem((2, 2 * keys, rope), bf16),
+            vmem((2, 2 * keys, span), jnp.int32),
             vmem((chunks, PAIR, span, nope), bf16),
-            dma((2,)), dma, dma, dma, dma, dma, dma, dma, dma,
+            dma((3,)), dma, dma, dma, dma, dma, dma, dma, dma,
             dma((chunks,)), dma((chunks,)),
-            dma((chunks, columns - 1)), dma((chunks, columns - 1)),
+            dma((chunks, columns - 1)), dma((chunks, columns)),
             dma((chunks,)), dma((chunks,)),
-            dma((chunks, columns - 1)), dma((chunks, columns - 1)),
-            dma((chunks,)), dma((chunks,)),
+            dma((chunks, columns)), dma((chunks, columns)),
+            dma((chunks,)), dma((chunks,)), dma((chunks,)), dma((chunks,)),
         ],
         compiler_params=pltpu.CompilerParams(
             collective_id=0, has_side_effects=True, vmem_limit_bytes=48 * 1024 * 1024
@@ -332,8 +402,8 @@
     shards = mesh.shape["ctx"]
     rope = latent_pages.shape[3] - w_keys.shape[0] * shards
     fits = (
-        mesh.shape["groups"] == 2 and mesh.shape["head"] == 2 and shards % 2 == 0
-        and shards >= 4 and w_keys.shape[0] % 16 == 0 and queries.shape[2] % (2 * PAIR) == 0
+        mesh.shape["groups"] == 2 and mesh.shape["head"] == 2 and shards % 4 == 0
+        and shards >= 8 and w_keys.shape[0] % 16 == 0 and queries.shape[2] % (2 * PAIR) == 0
         and w_keys.shape == w_values.shape and 2 * rope == w_keys.shape[2]
     )
     if fits:

time: 77.8 us -> 74.1 us (0.952)
  local copies, waits for them, and re-layouts: 7.15 us -> 4.08 us
    transpose x2 -> x0, local copies, waits for them, and re-layouts: 1.97 us -> none  [shared_on_device(): jnp.swapaxes(query[:, :, :nope], 0, 1).reshape(2, chunks, PAIR, span, nope)]
    slice x1 -> x0, local copies, waits for them, and re-layouts: 1.09 us -> none  [shared_on_device(): q_rope = query[:, :, nope:].reshape(span, heads // PAIR, nope)]
where the time goes in v2:
time: 74.1 us; the launch traced here: 73.9 us
  Pallas kernels  67.3 us (91%)
  local copies, waits for them, and re-layouts  4.08 us (6%)
  other arithmetic  1.71 us (2%)
  between operations  0.78 us (1%)
    pallas_call x1, Pallas kernels, shared_on_device(): pl.pallas_call(functools.partial(gather_attend, columns), out_shape=jax.S...  67.3 us
    reshape x1, local copies, waits for them, and re-layouts, shared_on_device(): return jnp.swapaxes(out.reshape(heads, span, nope), 0, 1)[None]  1.65 us

profile of v2, /device:TPU:0, one launch (start us, length us, event | category | flops | bytes accessed | tf_op | source)
XLA Modules:
  0.0 73.9 jit_solution(13920575540703306693)
XLA Ops:
  0.0 0.0 slice-start.1
  0.0 0.0 slice-start
  0.7 0.7 %select_reduce_fusion = s32[8]{0:T(128)S(1)} fusion(s32[8]{0:T(128)} %bitcast.38), kind=kLoop, calls=%fused_computation.6 | loop fusion | flops 184 | bytes 64 | tf_op jit(solution)/shard_map/reduce_sum | solution.py:368
  1.5 0.7 convert_bitcast_fusion
  2.1 0.0 copy-start.1
  2.1 0.0 copy-start.2
  2.2 0.1 copy.11
  2.3 0.3 mul.18
  2.6 0.0 slice-done.1
  2.6 0.1 fusion
  2.7 0.0 slice-done
  2.8 0.4 copy-done.1
  3.2 0.2 copy-done.2
  3.3 0.1 pad_maximum_fusion
  3.5 0.0 copy-start
  3.5 0.6 copy.12
  4.1 0.8 %copy-done = bf16[1,128,32,192]{1,3,2,0:T(8,128)(2,1)S(1)} copy-done((bf16[1,128,32,192]{1,3,2,0:T(8,128)(2,1)S(1)}, bf16[1,128,32,192]{1,3,2,0:T(8,128)(2,1)}, u32[]{:S(2)}) %copy-start) | copy-done | bytes 1572888
  4.9 67.3 %shard_map.73 = bf16[2,8,2,128,128]{4,3,2,1,0:T(8,128)(2,1)S(1)} custom-call(bf16[2,8,2,192,128]{4,3,2,1,0:T(8,128)(2,1)S(1)} %bitcast.33, bf16[256,576]{1,0:T(8,128)(2,1)S(1)} %pad_maximum_fusion.1.k_in, s32[8,8]{1,0:T(8,128)S(1)} %broadcast_in_dim.26.t_in, bf16[2,8,2,64,256]{4,3,2,1,0:T(8,128)(2,1)S(1)} %bitcast.31), custom_call_target="tpu_custom_call" | custom-call | tf_op jit(solution)/shard_map/pallas_call | solution.py:372
  72.2 1.6 %copy.17 = bf16[32,128,128]{2,0,1:T(8,128)(2,1)} copy(bf16[32,128,128]{2,1,0:T(8,128)(2,1)S(1)} %bitcast.32) | data formatting | bytes 2097152 | tf_op jit(solution)/shard_map/reshape | solution.py:397
  (3 shorter events, 0.0 us)
Async XLA Ops:
  0.0 2.6 %slice-start.1 = ((bf16[1,4,64,576]{3,2,1,0:T(8,128)(2,1)}), bf16[1,4,64,512]{3,2,1,0:T(8,128)(2,1)S(1)}, s32[]{:S(2)}) async-start(bf16[1,4,64,576]{3,2,1,0:T(8,128)(2,1)} %param.8), calls=%async_computation.1 | async-start | bytes 524288 | tf_op jit(solution)/shard_map/slice | solution.py:360
  0.0 2.7 %slice-start = ((bf16[1,4,64,576]{3,2,1,0:T(8,128)(2,1)}), bf16[1,4,64,64]{3,2,1,0:T(8,128)(2,1)S(1)}, s32[]{:S(2)}) async-start(bf16[1,4,64,576]{3,2,1,0:T(8,128)(2,1)} %param.8), calls=%async_computation | async-start | bytes 131072 | tf_op jit(solution)/shard_map/slice | solution.py:364
  2.1 1.0 %copy-start.1 = (bf16[64,32,128]{2,1,0:T(8,128)(2,1)S(1)}, bf16[64,32,128]{2,1,0:T(8,128)(2,1)}, u32[]{:S(2)}) copy-start(bf16[64,32,128]{2,1,0:T(8,128)(2,1)} %param.13) | copy-start | bytes 1572868
  2.1 1.2 %copy-start.2 = (bf16[64,32,128]{2,1,0:T(8,128)(2,1)S(1)}, bf16[64,32,128]{2,1,0:T(8,128)(2,1)}, u32[]{:S(2)}) copy-start(bf16[64,32,128]{2,1,0:T(8,128)(2,1)} %param.12) | copy-start | bytes 1572868
  3.5 1.4 %copy-start = (bf16[1,128,32,192]{1,3,2,0:T(8,128)(2,1)S(1)}, bf16[1,128,32,192]{1,3,2,0:T(8,128)(2,1)}, u32[]{:S(2)}) copy-start(bf16[1,128,32,192]{1,3,2,0:T(8,128)(2,1)} %param.7) | copy-start | bytes 4718596

commit v3 on v2

--- a/solution.py
+++ b/solution.py
@@ -10,7 +10,7 @@
 
 NEGATIVE = -1e30
 MESH = pl.DeviceIdType.MESH
-PAIR = 2
+PAIR = 4
 LAG = 1
 
 
@@ -159,12 +159,15 @@
 
     q_mine = pltpu.make_async_copy(q_in.at[y], q_own, own_sem.at[2])
     last = shard_columns - 1
-    relays = jnp.logical_or(row == 1, row == last - 1)
-    relay_source = jnp.where(row == 1, last, 0)
     partner = row + 1 - 2 * lax.rem(row, 2)
 
-    def far(other):
-        return jnp.abs(other - row) == last
+    others = [row + step * d for d in range(1, shard_columns) for step in (1, -1)]
+
+    def exists(other):
+        return jnp.logical_and(other >= 0, other <= last)
+
+    def onward(source):
+        return jnp.where(source < row, row + 1, row - 1)
 
     def block(c, source_row, source_side):
         return w_all.at[c, :, 2 * source_row + source_side]
@@ -172,10 +175,10 @@
     def q_copy(c):
         return remote(q_in.at[1 - y, c], q_rx.at[c], q_send.at[c], q_recv.at[c], y_peer)
 
-    def z_copy(c, d):
+    def z_copy(c, step):
         return remote(
-            w_in.at[y, c], block(c, row, side), z_send.at[c, d - 1], z_recv.at[c, row],
-            {"ctx": z_index(d)},
+            w_in.at[y, c], block(c, row, side), z_send.at[c, (step + 1) // 2], z_recv.at[c, row],
+            {"ctx": 2 * (row + step) + side},
         )
 
     def z_arrival(c, source):
@@ -183,11 +186,11 @@
             w_in.at[y, c], block(c, source, side), z_send.at[c, 0], z_recv.at[c, source], x_peer
         )
 
-    def r_copy(c):
-        moved = block(c, relay_source, side)
+    def r_copy(c, source):
+        moved = block(c, source, side)
         return remote(
-            moved, moved, r_send.at[c], z_recv.at[c, relay_source],
-            {"ctx": 2 * (last - relay_source) + side},
+            moved, moved, r_send.at[c, source], z_recv.at[c, source],
+            {"ctx": 2 * onward(source) + side},
         )
 
     def x_copy(c):
@@ -224,10 +227,11 @@
     w_own.start()
 
     def begin(c, carry):
-        for d in range(1, shard_columns):
-            @pl.when(jnp.logical_not(far(lax.rem(row + d, shard_columns))))
+        for step in (1, -1):
+            @pl.when(exists(row + step))
             def _():
-                z_copy(c, d).start()
+                z_copy(c, step).start()
+
         x_copy(c).start()
         q_copy(c).start()
         return carry
@@ -236,19 +240,18 @@
     k_own.wait()
     w_own.wait()
     q_mine.wait()
-    k_copy.wait_recv()
-    relay_copy.start()
-    t_copy.wait_recv()
-    core_copy.wait_recv()
-    relay_copy.wait_recv()
-    page = key_count // t_in.shape[1]
-    offset = lax.broadcasted_iota(jnp.int32, (page, span), 0)
-    offset = offset - lax.broadcasted_iota(jnp.int32, (page, span), 1)
-    for request, t_ref in ((y, t_in), (1 - y, t_rx)):
-        rot[request] = k_all[request, :, :, latent_width:].reshape(key_count, rope)
-        late[request] = jnp.concatenate(
-            [t_ref[0:1, p : p + 1] + offset for p in range(t_in.shape[1])], axis=0
-        )
+    def settle():
+        t_copy.wait_recv()
+        core_copy.wait_recv()
+        relay_copy.wait_recv()
+        page = key_count // t_in.shape[1]
+        offset = lax.broadcasted_iota(jnp.int32, (page, span), 0)
+        offset = offset - lax.broadcasted_iota(jnp.int32, (page, span), 1)
+        for request, t_ref in ((y, t_in), (1 - y, t_rx)):
+            rot[request] = k_all[request, :, :, latent_width:].reshape(key_count, rope)
+            late[request] = jnp.concatenate(
+                [t_ref[0:1, p : p + 1] + offset for p in range(t_in.shape[1])], axis=0
+            )
 
     def attend(c, request, q_ref, put):
         latent = k_all[request, :, :, :latent_width].reshape(key_count, latent_width)
@@ -277,17 +280,27 @@
             def _():
                 g_copy(c).start()
 
-            for d in range(1, shard_columns):
-                source = lax.rem(row + d, shard_columns)
-                z_arrival(c, source).wait_recv()
-
-                @pl.when(jnp.logical_and(relays, source == relay_source))
+            for source in others:
+                @pl.when(exists(source))
                 def _():
-                    r_copy(c).start()
-
-                @pl.when(over_x(c, source))
-                def _():
-                    f_copy(c, source).start()
+                    z_arrival(c, source).wait_recv()
+
+                    @pl.when(exists(onward(source)))
+                    def _():
+                        r_copy(c, source).start()
+
+                    @pl.when(over_x(c, source))
+                    def _():
+                        f_copy(c, source).start()
+
+        @pl.when(c == 0)
+        def _():
+            k_copy.wait_recv()
+            relay_copy.start()
+
+        @pl.when(c == LAG)
+        def _():
+            settle()
 
         @pl.when(c >= LAG)
         def _():
@@ -320,17 +333,18 @@
         for d in range(1, shard_columns):
             other = lax.rem(row + d, shard_columns)
 
-            @pl.when(jnp.logical_not(far(other)))
-            def _():
-                z_copy(c, d).wait_send()
-
             @pl.when(over_x(c, other))
             def _():
                 f_copy(c, other).wait_send()
 
-        @pl.when(relays)
-        def _():
-            r_copy(c).wait_send()
+            @pl.when(exists(onward(other)))
+            def _():
+                r_copy(c, other).wait_send()
+
+        for step in (1, -1):
+            @pl.when(exists(row + step))
+            def _():
+                z_copy(c, step).wait_send()
 
         @pl.when(lax.rem(c, 2) == 1)
         def _():
@@ -385,10 +399,10 @@
             vmem((chunks, PAIR, span, nope), bf16),
             dma((3,)), dma, dma, dma, dma, dma, dma, dma, dma,
             dma((chunks,)), dma((chunks,)),
-            dma((chunks, columns - 1)), dma((chunks, columns)),
+            dma((chunks, 2)), dma((chunks, columns)),
             dma((chunks,)), dma((chunks,)),
             dma((chunks, columns)), dma((chunks, columns)),
-            dma((chunks,)), dma((chunks,)), dma((chunks,)), dma((chunks,)),
+            dma((chunks, columns)), dma((chunks,)), dma((chunks,)), dma((chunks,)),
         ],
         compiler_params=pltpu.CompilerParams(
             collective_id=0, has_side_effects=True, vmem_limit_bytes=48 * 1024 * 1024

time: 74.1 us -> 71.7 us (0.968)
  Pallas kernels: 67.3 us -> 64.9 us
    pallas_call x1, Pallas kernels: 67.3 us -> 64.9 us  [shared_on_device(): pl.pallas_call(functools.partial(gather_attend, columns), out_shape=jax.S...]
where the time goes in v3:
time: 71.7 us; the launch traced here: 71.4 us
  Pallas kernels  64.9 us (91%)
  local copies, waits for them, and re-layouts  4.08 us (6%)
  other arithmetic  1.71 us (2%)
  between operations  0.78 us (1%)
    pallas_call x1, Pallas kernels, shared_on_device(): pl.pallas_call(functools.partial(gather_attend, columns), out_shape=jax.S...  64.9 us
    reshape x1, local copies, waits for them, and re-layouts, shared_on_device(): return jnp.swapaxes(out.reshape(heads, span, nope), 0, 1)[None]  1.65 us

profile of v3, /device:TPU:0, one launch (start us, length us, event | category | flops | bytes accessed | tf_op | source)
XLA Modules:
  0.0 71.4 jit_solution(5595060348822097087)
XLA Ops:
  0.0 0.0 slice-start.1
  0.0 0.0 slice-start
  0.7 0.7 %select_reduce_fusion = s32[8]{0:T(128)S(1)} fusion(s32[8]{0:T(128)} %bitcast.38), kind=kLoop, calls=%fused_computation.6 | loop fusion | flops 184 | bytes 64 | tf_op jit(solution)/shard_map/reduce_sum | solution.py:382
  1.5 0.7 convert_bitcast_fusion
  2.1 0.0 copy-start.1
  2.1 0.0 copy-start.2
  2.2 0.1 copy.11
  2.3 0.3 mul.18
  2.6 0.0 slice-done.1
  2.6 0.1 fusion
  2.7 0.0 slice-done
  2.8 0.4 copy-done.1
  3.2 0.2 copy-done.2
  3.3 0.1 pad_maximum_fusion
  3.5 0.0 copy-start
  3.5 0.6 copy.12
  4.1 0.8 %copy-done = bf16[1,128,32,192]{1,3,2,0:T(8,128)(2,1)S(1)} copy-done((bf16[1,128,32,192]{1,3,2,0:T(8,128)(2,1)S(1)}, bf16[1,128,32,192]{1,3,2,0:T(8,128)(2,1)}, u32[]{:S(2)}) %copy-start) | copy-done | bytes 1572888
  4.9 64.9 %shard_map.73 = bf16[2,4,4,128,128]{4,3,2,1,0:T(8,128)(2,1)S(1)} custom-call(bf16[2,4,4,192,128]{4,3,2,1,0:T(8,128)(2,1)S(1)} %bitcast.33, bf16[256,576]{1,0:T(8,128)(2,1)S(1)} %pad_maximum_fusion.1.k_in, s32[8,8]{1,0:T(8,128)S(1)} %broadcast_in_dim.26.t_in, bf16[2,4,4,64,256]{4,3,2,1,0:T(8,128)(2,1)S(1)} %bitcast.31), custom_call_target="tpu_custom_call" | custom-call | tf_op jit(solution)/shard_map/pallas_call | solution.py:386
  69.8 1.6 %copy.17 = bf16[32,128,128]{2,0,1:T(8,128)(2,1)} copy(bf16[32,128,128]{2,1,0:T(8,128)(2,1)S(1)} %bitcast.32) | data formatting | bytes 2097152 | tf_op jit(solution)/shard_map/reshape | solution.py:411
  (3 shorter events, 0.0 us)
Async XLA Ops:
  0.0 2.6 %slice-start.1 = ((bf16[1,4,64,576]{3,2,1,0:T(8,128)(2,1)}), bf16[1,4,64,512]{3,2,1,0:T(8,128)(2,1)S(1)}, s32[]{:S(2)}) async-start(bf16[1,4,64,576]{3,2,1,0:T(8,128)(2,1)} %param.8), calls=%async_computation.1 | async-start | bytes 524288 | tf_op jit(solution)/shard_map/slice | solution.py:374
  0.0 2.7 %slice-start = ((bf16[1,4,64,576]{3,2,1,0:T(8,128)(2,1)}), bf16[1,4,64,64]{3,2,1,0:T(8,128)(2,1)S(1)}, s32[]{:S(2)}) async-start(bf16[1,4,64,576]{3,2,1,0:T(8,128)(2,1)} %param.8), calls=%async_computation | async-start | bytes 131072 | tf_op jit(solution)/shard_map/slice | solution.py:378
  2.1 1.0 %copy-start.1 = (bf16[64,32,128]{2,1,0:T(8,128)(2,1)S(1)}, bf16[64,32,128]{2,1,0:T(8,128)(2,1)}, u32[]{:S(2)}) copy-start(bf16[64,32,128]{2,1,0:T(8,128)(2,1)} %param.13) | copy-start | bytes 1572868
  2.1 1.2 %copy-start.2 = (bf16[64,32,128]{2,1,0:T(8,128)(2,1)S(1)}, bf16[64,32,128]{2,1,0:T(8,128)(2,1)}, u32[]{:S(2)}) copy-start(bf16[64,32,128]{2,1,0:T(8,128)(2,1)} %param.12) | copy-start | bytes 1572868
  3.5 1.4 %copy-start = (bf16[1,128,32,192]{1,3,2,0:T(8,128)(2,1)S(1)}, bf16[1,128,32,192]{1,3,2,0:T(8,128)(2,1)}, u32[]{:S(2)}) copy-start(bf16[1,128,32,192]{1,3,2,0:T(8,128)(2,1)} %param.7) | copy-start | bytes 4718596
